TPU v7x, 32 devices: a whole 2x2x4 slice. The times are simulated.
32 devices in a mesh: grp: 2 (over y), row: 4 (over x, core), col: 4 (over z).
Axes of the slice: x: 2, y: 2, z: 4, core: 2. Of those that a mesh axis runs over, the one named last changes fastest.
Arguments:
- perturbation: bfloat16 [4, 12000, 12000], P('grp', 'row', 'col'), parts along dimension 0, may hold values from -96 to 96
- occ_coeffs: bfloat16 [12000, 2000], P('row', 'col'), may hold values from -0.0546875 to 0.0546875
- vir_coeffs: bfloat16 [12000, 512], P('col', 'row'), may hold values from -0.0546875 to 0.0546875
- occ_energies: float32 [2000], replicated, may hold values from -1 to -0.1
- vir_energies: float32 [512], replicated, may hold values from 0.1 to 1.5
Outputs:
- density_response: bfloat16 [4, 12000, 12000], P('grp', 'row', 'col'), parts along dimension 0
There are 2 independent parts, one for each index of `grp`. A program takes and returns all parts, laid end to end along the dimension named above; an argument that names none is the same for every part. Nothing has to cross between parts.
All inputs are finite; a program needn't handle non-finite values.
Results may differ from a plain program's by a relative error of at most 0.0098.
Values may be sent and summed in bfloat16 or wider, within the bound.
A program may use at most 192 MiB of HBM per device.

v0:
```python
import jax
import jax.numpy as jnp
from jax import lax
from jax.sharding import PartitionSpec as P


def per_device(perturbation, occ_coeffs, vir_coeffs, occ_energies, vir_energies):
    occ_rows = lax.all_gather(occ_coeffs, "col", axis=1, tiled=True)
    vir_rows = lax.all_gather(vir_coeffs, "row", axis=1, tiled=True)
    image = jnp.einsum("pij,jv->piv", perturbation, vir_rows, preferred_element_type=jnp.float32)
    image = lax.psum(image, "col")
    partial_value = jnp.einsum(
        "io,piv->pov", occ_rows.astype(jnp.float32), image, precision=lax.Precision.HIGHEST
    )
    coupling = lax.psum(partial_value, "row")
    gaps = occ_energies[:, None] - vir_energies[None, :]
    response = (coupling / gaps[None, :, :]).astype(jnp.bfloat16)
    mixed = jnp.einsum(
        "io,pov->piv", occ_rows, response, preferred_element_type=jnp.float32
    ).astype(jnp.bfloat16)
    return jnp.einsum("piv,jv->pij", mixed, vir_rows, preferred_element_type=jnp.float32).astype(
        jnp.bfloat16
    )


def solution(mesh):
    placed = (P("grp", "row", "col"), P("row", "col"), P("col", "row"), P(), P())
    return jax.shard_map(
        per_device, mesh=mesh, in_specs=placed, out_specs=P("grp", "row", "col"), check_vma=False
    )
```

profile of v0, /device:TPU:0, one launch (start us, length us, event | category | flops | bytes accessed | tf_op | source)
XLA Modules:
  0.0 920.3 jit_solution(8147711302796807755)
XLA Ops:
  6.5 0.0 all-gather.4.cloned.1.call-start
  6.5 0.7 all-gather.4.cloned.1.call-update
  7.3 0.0 all-gather.6.cloned.1.call-start
  7.3 0.7 all-gather.6.cloned.1.call-update
  8.0 0.0 all-reduce.3.cloned.1.call-start
  8.1 32.1 %all-gather.4.cloned.1.call-done = bf16[3000,512]{1,0:T(8,128)(2,1)} async-done(((bf16[3000,128]{1,0:T(8,128)(2,1)}), bf16[3000,512]{1,0:T(8,128)(2,1)}) %all-gather.4.cloned.1.call-update) | async-done | bytes 3072016 | tf_op jit(solution)/shard_map/all_gather | solution.py:9
  40.1 26.8 %fusion.6 = f32[2,3000,512]{2,1,0:T(8,128)} fusion(bf16[2,3000,3000]{2,1,0:T(8,128)(2,1)} %param.5, bf16[3000,512]{1,0:T(8,128)(2,1)} %all-gather.4.cloned.1.call-done), kind=kOutput, calls=%fused_computation.9 | convolution fusion | flops 18432000000 | bytes 51360000 | tf_op jit(solution)/shard_map/pij,jv->piv/dot_general | solution.py:10
  66.9 0.0 all-reduce.3.cloned.1.call-update
  66.9 0.0 all-reduce.5.cloned.1.call-start
  67.0 188.1 %all-gather.6.cloned.1.call-done = bf16[4,500,3000]{1,2,0:T(8,128)(2,1)} async-done(((bf16[1,500,3000]{1,2,0:T(8,128)(2,1)}), bf16[4,500,3000]{1,2,0:T(8,128)(2,1)}) %all-gather.6.cloned.1.call-update) | async-done | bytes 12000016 | tf_op jit(solution)/shard_map/all_gather | solution.py:8
  255.1 16.1 %copy.7 = bf16[4,500,3000]{2,1,0:T(8,128)(2,1)} copy(bf16[4,500,3000]{1,2,0:T(8,128)(2,1)} %all-gather.6.cloned.1.call-done) | data formatting | bytes 24000000 | tf_op jit(solution)/shard_map/all_gather | solution.py:8
  271.2 16.2 %reshape.30 = bf16[2000,3000,1]{1,0,2:T(8,128)(2,1)} reshape(bf16[4,500,3000]{2,1,0:T(8,128)(2,1)} %copy.7) | data formatting | bytes 24000000
  287.4 385.4 %all-reduce.3.cloned.1.call-done = f32[2,3000,512]{2,1,0:T(8,128)} async-done(((f32[2,3000,512]{2,1,0:T(8,128)}), f32[2,3000,512]{2,1,0:T(8,128)}) %all-reduce.3.cloned.1.call-update) | async-done | bytes 12288016 | tf_op jit(solution)/shard_map/psum | solution.py:11
  672.7 44.9 %convolution_bitcast_fusion = f32[2,2000,512]{2,1,0:T(8,128)} fusion(f32[2,3000,512]{2,1,0:T(8,128)} %all-reduce.3.cloned.1.call-done, bf16[2000,3000,1]{1,0,2:T(8,128)(2,1)} %reshape.30), kind=kOutput, calls=%fused_computation.6 | convolution fusion | flops 73728000000 | bytes 32480000 | tf_op jit(solution)/shard_map/io,piv->pov/dot_general | solution.py:12
  717.7 0.0 copy-start
  717.7 0.0 copy-start.1
  717.7 0.0 all-reduce.5.cloned.1.call-update
  717.7 0.7 copy-done
  718.4 0.0 copy-done.1
  718.4 2.3 broadcast_subtract_fusion
  720.7 17.0 %reshape.28 = bf16[2000,3000]{1,0:T(8,128)(2,1)} reshape(bf16[4,500,3000]{2,1,0:T(8,128)(2,1)} %copy.7) | data formatting | bytes 24000000
  737.7 0.0 copy-start.2
  737.7 128.8 %all-reduce.5.cloned.1.call-done = f32[2,2000,512]{2,1,0:T(8,128)} async-done(((f32[2,2000,512]{2,1,0:T(8,128)}), f32[2,2000,512]{2,1,0:T(8,128)}) %all-reduce.5.cloned.1.call-update) | async-done | bytes 8192016 | tf_op jit(solution)/shard_map/psum | solution.py:15
  866.5 20.9 %fusion = bf16[2,512,3000]{1,2,0:T(8,128)(2,1)} fusion(bf16[2000,3000]{1,0:T(8,128)(2,1)} %reshape.28, f32[2,2000,512]{2,1,0:T(8,128)} %all-reduce.5.cloned.1.call-done, f32[2000,512]{1,0:T(8,128)} %broadcast_subtract_fusion), kind=kOutput, calls=%fused_computation.1 | convolution fusion | flops 12292096000 | bytes 30432000 | tf_op jit(solution)/shard_map/io,pov->piv/dot_general | solution.py:18
  887.3 0.0 copy-done.2
  887.3 26.4 %convolution_convert_fusion = bf16[2,3000,3000]{2,1,0:T(8,128)(2,1)} fusion(bf16[2,512,3000]{1,2,0:T(8,128)(2,1)} %fusion, bf16[3000,512]{1,0:T(8,128)(2,1)S(1)} %copy-done.2), kind=kOutput, calls=%fused_computation | convolution fusion | flops 18449999872 | bytes 45216000 | tf_op jit(solution)/shard_map/piv,jv->pij/dot_general | solution.py:21
Async XLA Ops:
  6.5 33.6 %all-gather.4.cloned.1.call-start = ((), (), s32[]{:S(2)}) async-start(), calls=%async_computation | async-start | bytes 3840000 | tf_op jit(solution)/shard_map/all_gather | solution.py:9
  7.3 247.8 %all-gather.6.cloned.1.call-start = ((), (), s32[]{:S(2)}) async-start(), calls=%async_computation.3 | async-start | bytes 15360000 | tf_op jit(solution)/shard_map/all_gather | solution.py:8
  8.0 664.7 %all-reduce.3.cloned.1.call-start = ((), (), s32[]{:S(2)}) async-start(), calls=%async_computation.1 | async-start | bytes 24576000 | tf_op jit(solution)/shard_map/psum | solution.py:11
  66.9 799.5 %all-reduce.5.cloned.1.call-start = ((), (), s32[]{:S(2)}) async-start(), calls=%async_computation.2 | async-start | bytes 16384000 | tf_op jit(solution)/shard_map/psum | solution.py:15
  717.7 0.7 copy-start
  717.7 0.7 copy-start.1
  737.7 149.7 %copy-start.2 = (bf16[3000,512]{1,0:T(8,128)(2,1)S(1)}, bf16[3000,512]{1,0:T(8,128)(2,1)}, u32[]{:S(2)}) copy-start(bf16[3000,512]{1,0:T(8,128)(2,1)} %all-gather.4.cloned.1.call-done) | copy-start | bytes 9216004
Sparse Core Ops, SparseCore 0:
  8.9 31.1 all-gather.3
  41.7 213.3 all-gather.5
  257.6 415.1 all-reduce.2
  717.8 148.6 all-reduce.4
where the time goes:
time: 921 us; the launch traced here: 920 us
  waiting for transfers between devices  736 us (80%)
  matrix products  119 us (13%)
  local copies, waits for them, and re-layouts  50 us (5%)
  between operations  13.1 us (1%)
    psum x1, waiting for transfers between devices, per_device(): image = lax.psum(image, 'col')  385 us
    all_gather x1, waiting for transfers between devices, per_device(): occ_rows = lax.all_gather(occ_coeffs, 'col', axis=1, tiled=True)  188 us
    psum x1, waiting for transfers between devices, per_device(): coupling = lax.psum(partial_value, 'row')  129 us
    dot_general x1, matrix products, per_device(): jnp.einsum('io,piv->pov', occ_rows.astype(jnp.float32), image, precision=...  44.9 us
    unnamed x8, local copies, waits for them, and re-layouts  33.9 us
    all_gather x1, waiting for transfers between devices, per_device(): vir_rows = lax.all_gather(vir_coeffs, 'row', axis=1, tiled=True)  32.1 us
    dot_general x1, matrix products, per_device(): jnp.einsum('pij,jv->piv', perturbation, vir_rows, preferred_element_type=...  26.8 us
    dot_general x1, matrix products, per_device(): jnp.einsum('piv,jv->pij', mixed, vir_rows, preferred_element_type=jnp.flo...  26.4 us
  transfers between devices with their start and end apart: 4, of which 4 were waited for; matrix products, arithmetic and copies ran while one was open for 9% of the time, Pallas kernels for 0%

commit v1 on v0

--- a/solution.py
+++ b/solution.py
@@ -4,11 +4,20 @@
 from jax.sharding import PartitionSpec as P
 
 
+def add_in_pairs(value, mesh_axis):
+    n_dev = lax.axis_size(mesh_axis)
+    total, far = (value, 1)
+    while far < n_dev:
+        total = total + lax.ppermute(total, mesh_axis, [(i, i ^ far) for i in range(n_dev)])
+        far = 2 * far
+    return total
+
+
 def per_device(perturbation, occ_coeffs, vir_coeffs, occ_energies, vir_energies):
     occ_rows = lax.all_gather(occ_coeffs, "col", axis=1, tiled=True)
     vir_rows = lax.all_gather(vir_coeffs, "row", axis=1, tiled=True)
     image = jnp.einsum("pij,jv->piv", perturbation, vir_rows, preferred_element_type=jnp.float32)
-    image = lax.psum(image, "col")
+    image = add_in_pairs(image, "col")
     partial_value = jnp.einsum(
         "io,piv->pov", occ_rows.astype(jnp.float32), image, precision=lax.Precision.HIGHEST
     )

time: 921 us -> 1330 us (1.44)
  waiting for transfers between devices: 736 us -> 1120 us
  other arithmetic: 2.29 us -> 16.4 us
    ppermute x0 -> x2, waiting for transfers between devices: none -> 957 us  [add_in_pairs(): lax.ppermute(total, mesh_axis, [(i, i ^ far) for i in range(n_dev)])]
    psum x1 -> x0, waiting for transfers between devices: 385 us -> none  [per_device(): image = lax.psum(image, 'col')]
    all_gather x1, waiting for transfers between devices: 188 us -> 0.01 us  [per_device(): occ_rows = lax.all_gather(occ_coeffs, 'col', axis=1, tiled=True)]
    add x0 -> x1, other arithmetic: none -> 14.1 us  [add_in_pairs(): total + lax.ppermute(total, mesh_axis, [(i, i ^ far) for i in range(n_dev)])]
  transfers between devices with their start and end apart: 4 -> 5, of which waited for: 4 -> 4; matrix products, arithmetic and copies ran while one was open for 9% -> 5% of each run, Pallas kernels for 0% -> 0%
where the time goes in v1:
time: 1330 us
  waiting for transfers between devices  1120 us (84%)
  matrix products  123 us (9%)
  local copies, waits for them, and re-layouts  49.1 us (4%)
  other arithmetic  16.4 us (1%)
  between operations  14.9 us (1%)
    ppermute x2, waiting for transfers between devices, add_in_pairs(): lax.ppermute(total, mesh_axis, [(i, i ^ far) for i in range(n_dev)])  957 us
    psum x1, waiting for transfers between devices, per_device(): coupling = lax.psum(partial_value, 'row')  131 us
    dot_general x1, matrix products, per_device(): jnp.einsum('io,piv->pov', occ_rows.astype(jnp.float32), image, precision=...  49.8 us
    all_gather x1, waiting for transfers between devices, per_device(): vir_rows = lax.all_gather(vir_coeffs, 'row', axis=1, tiled=True)  32.8 us
    unnamed x8, local copies, waits for them, and re-layouts  32.4 us
  transfers between devices with their start and end apart: 5, of which 4 were waited for; matrix products, arithmetic and copies ran while one was open for 5% of the time, Pallas kernels for 0%

profile of v1, /device:TPU:0, one launch (start us, length us, event | category | flops | bytes accessed | tf_op | source)
XLA Modules:
  0.0 1329.4 jit_solution(4852278888481968248)
XLA Ops:
  7.4 0.0 all-gather.4.cloned.1.call-start
  7.4 0.7 all-gather.4.cloned.1.call-update
  8.1 0.0 all-gather.6.cloned.1.call-start
  8.1 32.8 %all-gather.4.cloned.1.call-done = bf16[3000,512]{1,0:T(8,128)(2,1)} async-done(((bf16[3000,128]{1,0:T(8,128)(2,1)}), bf16[3000,512]{1,0:T(8,128)(2,1)}) %all-gather.4.cloned.1.call-update) | async-done | bytes 3072016 | tf_op jit(solution)/shard_map/all_gather | solution.py:18
  40.9 26.1 %fusion.11 = f32[2,3000,512]{2,1,0:T(8,128)} fusion(bf16[2,3000,3000]{2,1,0:T(8,128)(2,1)} %param.5, bf16[3000,512]{1,0:T(8,128)(2,1)} %all-gather.4.cloned.1.call-done), kind=kOutput, calls=%fused_computation.11 | convolution fusion | flops 18432000000 | bytes 51360000 | tf_op jit(solution)/shard_map/pij,jv->piv/dot_general | solution.py:19
  67.0 1.5 collective-permute-start
  68.5 0.0 all-gather.6.cloned.1.call-update
  68.5 0.0 all-reduce.2.cloned.1.call-start
  68.6 462.4 %collective-permute-done = f32[2,3000,512]{2,1,0:T(8,128)} collective-permute-done((f32[2,3000,512]{2,1,0:T(8,128)}, f32[2,3000,512]{2,1,0:T(8,128)}, u32[]{:S(2)}, u32[]{:S(2)}) %collective-permute-start) | collective-permute-done | bytes 12288032 | tf_op jit(solution)/shard_map/ppermute | solution.py:11
  531.0 14.1 %add.8 = f32[2,3000,512]{2,1,0:T(8,128)} add(f32[2,3000,512]{2,1,0:T(8,128)} %fusion.11, f32[2,3000,512]{2,1,0:T(8,128)} %collective-permute-done) | non-fusion elementwise | flops 3072000 | bytes 36864000 | tf_op jit(solution)/shard_map/add | solution.py:11
  545.1 2.4 collective-permute-start.1
  547.5 0.0 all-gather.6.cloned.1.call-done
  547.5 16.7 %copy.7 = bf16[4,500,3000]{2,1,0:T(8,128)(2,1)} copy(bf16[4,500,3000]{1,2,0:T(8,128)(2,1)} %all-gather.6.cloned.1.call-done) | data formatting | bytes 24000000 | tf_op jit(solution)/shard_map/all_gather | solution.py:17
  564.2 16.2 %reshape.30 = bf16[2000,3000,1]{1,0,2:T(8,128)(2,1)} reshape(bf16[4,500,3000]{2,1,0:T(8,128)(2,1)} %copy.7) | data formatting | bytes 24000000
  580.3 0.0 copy-start
  580.3 0.0 copy-start.1
  580.4 494.6 %collective-permute-done.1 = f32[2,3000,512]{2,1,0:T(8,128)} collective-permute-done((f32[2,3000,512]{2,1,0:T(8,128)}, f32[2,3000,512]{2,1,0:T(8,128)}, u32[]{:S(2)}, u32[]{:S(2)}) %collective-permute-start.1) | collective-permute-done | bytes 12288032 | tf_op jit(solution)/shard_map/ppermute | solution.py:11
  1074.9 49.8 %fusion.6 = f32[2,2000,512]{2,1,0:T(8,128)} fusion(bf16[2000,3000,1]{1,0,2:T(8,128)(2,1)} %reshape.30, f32[2,3000,512]{2,1,0:T(8,128)} %add.8, f32[2,3000,512]{2,1,0:T(8,128)} %collective-permute-done.1), kind=kOutput, calls=%fused_computation.8 | convolution fusion | flops 73731072000 | bytes 44768000 | tf_op jit(solution)/shard_map/io,piv->pov/dot_general | solution.py:21
  1124.7 0.0 all-reduce.2.cloned.1.call-update
  1124.8 0.0 copy-done
  1124.8 0.0 copy-done.1
  1124.8 2.4 broadcast_subtract_fusion
  1127.2 16.2 %reshape.28 = bf16[2000,3000]{1,0:T(8,128)(2,1)} reshape(bf16[4,500,3000]{2,1,0:T(8,128)(2,1)} %copy.7) | data formatting | bytes 24000000
  1143.4 0.0 copy-start.2
  1143.4 131.2 %all-reduce.2.cloned.1.call-done = f32[2,2000,512]{2,1,0:T(8,128)} async-done(((f32[2,2000,512]{2,1,0:T(8,128)}), f32[2,2000,512]{2,1,0:T(8,128)}) %all-reduce.2.cloned.1.call-update) | async-done | bytes 8192016 | tf_op jit(solution)/shard_map/psum | solution.py:24
  1274.6 20.9 %fusion = bf16[2,512,3000]{1,2,0:T(8,128)(2,1)} fusion(bf16[2000,3000]{1,0:T(8,128)(2,1)} %reshape.28, f32[2,2000,512]{2,1,0:T(8,128)} %all-reduce.2.cloned.1.call-done, f32[2000,512]{1,0:T(8,128)} %broadcast_subtract_fusion), kind=kOutput, calls=%fused_computation.1 | convolution fusion | flops 12292096000 | bytes 30432000 | tf_op jit(solution)/shard_map/io,pov->piv/dot_general | solution.py:27
  1295.5 0.0 copy-done.2
  1295.5 26.4 %convolution_convert_fusion = bf16[2,3000,3000]{2,1,0:T(8,128)(2,1)} fusion(bf16[2,512,3000]{1,2,0:T(8,128)(2,1)} %fusion, bf16[3000,512]{1,0:T(8,128)(2,1)S(1)} %copy-done.2), kind=kOutput, calls=%fused_computation | convolution fusion | flops 18449999872 | bytes 45216000 | tf_op jit(solution)/shard_map/piv,jv->pij/dot_general | solution.py:30
Async XLA Ops:
  7.4 33.6 %all-gather.4.cloned.1.call-start = ((), (), s32[]{:S(2)}) async-start(), calls=%async_computation | async-start | bytes 3840000 | tf_op jit(solution)/shard_map/all_gather | solution.py:18
  8.1 539.4 %all-gather.6.cloned.1.call-start = ((), (), s32[]{:S(2)}) async-start(), calls=%async_computation.2 | async-start | bytes 15360000 | tf_op jit(solution)/shard_map/all_gather | solution.py:17
  67.0 464.0 %collective-permute-start = (f32[2,3000,512]{2,1,0:T(8,128)}, f32[2,3000,512]{2,1,0:T(8,128)}, u32[]{:S(2)}, u32[]{:S(2)}) collective-permute-start(f32[2,3000,512]{2,1,0:T(8,128)} %fusion.11), channel_id=1, source_target_pairs={{0,1},{1,0},{2,3},{3,2},{4,5},{5,4},{6,7},{7,6},{8,9},{9,8},{10,11... | collective-permute-start | bytes 36864008 | tf_op jit(solution)/shard_map/ppermute | solution.py:11
  68.5 1206.0 %all-reduce.2.cloned.1.call-start = ((), (), s32[]{:S(2)}) async-start(), calls=%async_computation.1 | async-start | bytes 16384000 | tf_op jit(solution)/shard_map/psum | solution.py:24
  545.1 529.9 %collective-permute-start.1 = (f32[2,3000,512]{2,1,0:T(8,128)}, f32[2,3000,512]{2,1,0:T(8,128)}, u32[]{:S(2)}, u32[]{:S(2)}) collective-permute-start(f32[2,3000,512]{2,1,0:T(8,128)} %add.8), channel_id=1, source_target_pairs={{0,2},{1,3},{2,0},{3,1},{4,6},{5,7},{6,4},{7,5},{8,10},{9,11},{10,... | collective-permute-start | bytes 36864008 | tf_op jit(solution)/shard_map/ppermute | solution.py:11
  580.3 544.4 %copy-start = (f32[2000]{0:T(1024)S(1)}, f32[2000]{0:T(1024)}, u32[]{:S(2)}) copy-start(f32[2000]{0:T(1024)} %param.8) | copy-start | bytes 24004
  580.3 544.4 %copy-start.1 = (f32[512]{0:T(512)S(1)}, f32[512]{0:T(512)}, u32[]{:S(2)}) copy-start(f32[512]{0:T(512)} %param.9) | copy-start | bytes 6148
  1143.4 152.1 %copy-start.2 = (bf16[3000,512]{1,0:T(8,128)(2,1)S(1)}, bf16[3000,512]{1,0:T(8,128)(2,1)}, u32[]{:S(2)}) copy-start(bf16[3000,512]{1,0:T(8,128)(2,1)} %all-gather.4.cloned.1.call-done) | copy-start | bytes 9216004
Sparse Core Ops, SparseCore 0:
  9.7 31.1 all-gather.3
  1124.9 149.6 all-reduce.1
Sparse Core Ops, SparseCore 1:
  68.6 405.1 all-gather.5

commit v2 on v0

--- a/solution.py
+++ b/solution.py
@@ -12,7 +12,10 @@
     partial_value = jnp.einsum(
         "io,piv->pov", occ_rows.astype(jnp.float32), image, precision=lax.Precision.HIGHEST
     )
-    coupling = lax.psum(partial_value, "row")
+    size, coupling = (lax.axis_size("row"), partial_value)
+    for far in [1 << k for k in range(size.bit_length() - 1)]:
+        swap = [(i, i ^ far) for i in range(size)]
+        coupling = coupling + lax.ppermute(coupling, "row", swap)
     gaps = occ_energies[:, None] - vir_energies[None, :]
     response = (coupling / gaps[None, :, :]).astype(jnp.bfloat16)
     mixed = jnp.einsum(

time: 921 us -> 976 us (1.060)
  waiting for transfers between devices: 736 us -> 778 us
    ppermute x0 -> x2, waiting for transfers between devices: none -> 172 us  [per_device(): coupling = coupling + lax.ppermute(coupling, 'row', swap)]
    psum x1 -> x0, waiting for transfers between devices: 129 us -> none  [per_device(): coupling = lax.psum(partial_value, 'row')]
  transfers between devices with their start and end apart: 4 -> 5, of which waited for: 4 -> 5; matrix products, arithmetic and copies ran while one was open for 9% -> 8% of each run, Pallas kernels for 0% -> 0%
where the time goes in v2:
time: 976 us; the launch traced here: 975 us
  waiting for transfers between devices  778 us (80%)
  matrix products  122 us (12%)
  local copies, waits for them, and re-layouts  48.5 us (5%)
  between operations  13.1 us (1%)
  other arithmetic  10.9 us (1%)
    psum x1, waiting for transfers between devices, per_device(): image = lax.psum(image, 'col')  385 us
    all_gather x1, waiting for transfers between devices, per_device(): occ_rows = lax.all_gather(occ_coeffs, 'col', axis=1, tiled=True)  188 us
    ppermute x2, waiting for transfers between devices, per_device(): coupling = coupling + lax.ppermute(coupling, 'row', swap)  172 us
    dot_general x1, matrix products, per_device(): jnp.einsum('io,piv->pov', occ_rows.astype(jnp.float32), image, precision=...  45.6 us
    unnamed x8, local copies, waits for them, and re-layouts  32.3 us
    all_gather x1, waiting for transfers between devices, per_device(): vir_rows = lax.all_gather(vir_coeffs, 'row', axis=1, tiled=True)  32.1 us
    dot_general x1, matrix products, per_device(): jnp.einsum('pij,jv->piv', perturbation, vir_rows, preferred_element_type=...  26.9 us
    dot_general x1, matrix products, per_device(): jnp.einsum('piv,jv->pij', mixed, vir_rows, preferred_element_type=jnp.flo...  26.4 us
  transfers between devices with their start and end apart: 5, of which 5 were waited for; matrix products, arithmetic and copies ran while one was open for 8% of the time, Pallas kernels for 0%

profile of v2, /device:TPU:0, one launch (start us, length us, event | category | flops | bytes accessed | tf_op | source)
XLA Modules:
  0.0 975.0 jit_solution(6560987757880370045)
XLA Ops:
  6.5 0.0 all-gather.4.cloned.1.call-start
  6.5 0.7 all-gather.4.cloned.1.call-update
  7.3 0.0 all-gather.6.cloned.1.call-start
  7.3 0.7 all-gather.6.cloned.1.call-update
  8.0 0.0 all-reduce.2.cloned.1.call-start
  8.1 32.1 %all-gather.4.cloned.1.call-done = bf16[3000,512]{1,0:T(8,128)(2,1)} async-done(((bf16[3000,128]{1,0:T(8,128)(2,1)}), bf16[3000,512]{1,0:T(8,128)(2,1)}) %all-gather.4.cloned.1.call-update) | async-done | bytes 3072016 | tf_op jit(solution)/shard_map/all_gather | solution.py:9
  40.1 26.9 %fusion.6 = f32[2,3000,512]{2,1,0:T(8,128)} fusion(bf16[2,3000,3000]{2,1,0:T(8,128)(2,1)} %param.5, bf16[3000,512]{1,0:T(8,128)(2,1)} %all-gather.4.cloned.1.call-done), kind=kOutput, calls=%fused_computation.9 | convolution fusion | flops 18432000000 | bytes 51360000 | tf_op jit(solution)/shard_map/pij,jv->piv/dot_general | solution.py:10
  67.0 0.0 all-reduce.2.cloned.1.call-update
  67.1 188.0 %all-gather.6.cloned.1.call-done = bf16[4,500,3000]{1,2,0:T(8,128)(2,1)} async-done(((bf16[1,500,3000]{1,2,0:T(8,128)(2,1)}), bf16[4,500,3000]{1,2,0:T(8,128)(2,1)}) %all-gather.6.cloned.1.call-update) | async-done | bytes 12000016 | tf_op jit(solution)/shard_map/all_gather | solution.py:8
  255.1 16.1 %copy.8 = bf16[4,500,3000]{2,1,0:T(8,128)(2,1)} copy(bf16[4,500,3000]{1,2,0:T(8,128)(2,1)} %all-gather.6.cloned.1.call-done) | data formatting | bytes 24000000 | tf_op jit(solution)/shard_map/all_gather | solution.py:8
  271.2 16.2 %reshape.30 = bf16[2000,3000,1]{1,0,2:T(8,128)(2,1)} reshape(bf16[4,500,3000]{2,1,0:T(8,128)(2,1)} %copy.8) | data formatting | bytes 24000000
  287.4 385.4 %all-reduce.2.cloned.1.call-done = f32[2,3000,512]{2,1,0:T(8,128)} async-done(((f32[2,3000,512]{2,1,0:T(8,128)}), f32[2,3000,512]{2,1,0:T(8,128)}) %all-reduce.2.cloned.1.call-update) | async-done | bytes 12288016 | tf_op jit(solution)/shard_map/psum | solution.py:11
  672.7 45.6 %convolution_bitcast_fusion = f32[2,2000,512]{2,1,0:T(8,128)S(1)} fusion(f32[2,3000,512]{2,1,0:T(8,128)} %all-reduce.2.cloned.1.call-done, bf16[2000,3000,1]{1,0,2:T(8,128)(2,1)} %reshape.30), kind=kOutput, calls=%fused_computation.6 | convolution fusion | flops 73728000000 | bytes 32480000 | tf_op jit(solution)/shard_map/io,piv->pov/dot_general | solution.py:12
  718.3 0.0 copy-start
  718.4 0.0 copy-start.1
  718.4 0.1 collective-permute-start
  718.4 13.0 %collective-permute-done = f32[2,2000,512]{2,1,0:T(8,128)} collective-permute-done((f32[2,2000,512]{2,1,0:T(8,128)S(1)}, f32[2,2000,512]{2,1,0:T(8,128)}, u32[]{:S(2)}, u32[]{:S(2)}) %collective-permute-start) | collective-permute-done | bytes 8192032 | tf_op jit(solution)/shard_map/ppermute | solution.py:18
  731.4 8.5 add.8
  740.0 1.5 collective-permute-start.1
  741.4 0.0 copy-done
  741.4 0.0 copy-done.1
  741.4 2.3 broadcast_subtract_fusion
  743.8 16.2 %reshape.28 = bf16[2000,3000]{1,0:T(8,128)(2,1)} reshape(bf16[4,500,3000]{2,1,0:T(8,128)(2,1)} %copy.8) | data formatting | bytes 24000000
  759.9 0.0 copy-start.2
  759.9 158.6 %collective-permute-done.1 = f32[2,2000,512]{2,1,0:T(8,128)} collective-permute-done((f32[2,2000,512]{2,1,0:T(8,128)}, f32[2,2000,512]{2,1,0:T(8,128)}, u32[]{:S(2)}, u32[]{:S(2)}) %collective-permute-start.1) | collective-permute-done | bytes 8192032 | tf_op jit(solution)/shard_map/ppermute | solution.py:18
  918.6 23.4 %fusion = bf16[2,512,3000]{1,2,0:T(8,128)(2,1)} fusion(bf16[2000,3000]{1,0:T(8,128)(2,1)} %reshape.28, f32[2,2000,512]{2,1,0:T(8,128)} %add.8, f32[2,2000,512]{2,1,0:T(8,128)} %collective-permute-done.1, f32[2000,512]{1,0:T(8,128)} %broadcast_subtract_fusion), kind=kOutput, calls=%fused_computation.1 | convolution fusion | flops 12294144000 | bytes 38624000 | tf_op jit(solution)/shard_map/io,pov->piv/dot_general | solution.py:21
  942.0 0.0 copy-done.2
  942.0 26.4 %convolution_convert_fusion = bf16[2,3000,3000]{2,1,0:T(8,128)(2,1)} fusion(bf16[2,512,3000]{1,2,0:T(8,128)(2,1)} %fusion, bf16[3000,512]{1,0:T(8,128)(2,1)S(1)} %copy-done.2), kind=kOutput, calls=%fused_computation | convolution fusion | flops 18449999872 | bytes 45216000 | tf_op jit(solution)/shard_map/piv,jv->pij/dot_general | solution.py:24
Async XLA Ops:
  6.5 33.6 %all-gather.4.cloned.1.call-start = ((), (), s32[]{:S(2)}) async-start(), calls=%async_computation | async-start | bytes 3840000 | tf_op jit(solution)/shard_map/all_gather | solution.py:9
  7.3 247.8 %all-gather.6.cloned.1.call-start = ((), (), s32[]{:S(2)}) async-start(), calls=%async_computation.2 | async-start | bytes 15360000 | tf_op jit(solution)/shard_map/all_gather | solution.py:8
  8.0 664.7 %all-reduce.2.cloned.1.call-start = ((), (), s32[]{:S(2)}) async-start(), calls=%async_computation.1 | async-start | bytes 24576000 | tf_op jit(solution)/shard_map/psum | solution.py:11
  718.3 23.1 %copy-start = (f32[2000]{0:T(1024)S(1)}, f32[2000]{0:T(1024)}, u32[]{:S(2)}) copy-start(f32[2000]{0:T(1024)} %param.8) | copy-start | bytes 24004
  718.4 23.1 %copy-start.1 = (f32[512]{0:T(512)S(1)}, f32[512]{0:T(512)}, u32[]{:S(2)}) copy-start(f32[512]{0:T(512)} %param.9) | copy-start | bytes 6148
  718.4 13.1 %collective-permute-start = (f32[2,2000,512]{2,1,0:T(8,128)S(1)}, f32[2,2000,512]{2,1,0:T(8,128)}, u32[]{:S(2)}, u32[]{:S(2)}) collective-permute-start(f32[2,2000,512]{2,1,0:T(8,128)S(1)} %convolution_bitcast_fusion), channel_id=1, source_target_pairs={{0,4},{4,0},{8,12},{12,8},{1,5},{5,1},{9,13},{13,9},{2,6},{6,2},{1... | collective-permute-start | bytes 24576008 | tf_op jit(solution)/shard_map/ppermute | solution.py:18
  740.0 178.6 %collective-permute-start.1 = (f32[2,2000,512]{2,1,0:T(8,128)}, f32[2,2000,512]{2,1,0:T(8,128)}, u32[]{:S(2)}, u32[]{:S(2)}) collective-permute-start(f32[2,2000,512]{2,1,0:T(8,128)} %add.8), channel_id=1, source_target_pairs={{0,8},{4,12},{8,0},{12,4},{1,9},{5,13},{9,1},{13,5},{2,10},{6,14},... | collective-permute-start | bytes 24576008 | tf_op jit(solution)/shard_map/ppermute | solution.py:18
  759.9 182.0 %copy-start.2 = (bf16[3000,512]{1,0:T(8,128)(2,1)S(1)}, bf16[3000,512]{1,0:T(8,128)(2,1)}, u32[]{:S(2)}) copy-start(bf16[3000,512]{1,0:T(8,128)(2,1)} %all-gather.4.cloned.1.call-done) | copy-start | bytes 9216004
Sparse Core Ops, SparseCore 0:
  8.9 31.1 all-gather.3
  41.7 213.3 all-gather.5
  257.6 415.1 all-reduce.1
